TPU v7x, 32 devices: a whole 2x2x4 slice. The times are simulated.
32 devices in a mesh: tp: 4 (over y, core), dp: 8 (over z, x).
Axes of the slice: x: 2, y: 2, z: 4, core: 2. Of those that a mesh axis runs over, the one named last changes fastest.
Arguments:
- teacher_query: bfloat16 [8192, 8192], P('dp', 'tp'), may hold values from -8 to 8
- student_hidden: bfloat16 [8192, 4096], P('dp', 'tp'), may hold values from -16 to 16
- query_weight: bfloat16 [4096, 4096], P('dp', 'tp'), may hold values from -0.039794922 to 0.039794922
Outputs:
- kl_rows: float32 [32, 8192], P(('tp', 'dp'))
- weight_grad: float32 [4096, 4096], P('dp', 'tp')
All inputs are finite; a program needn't handle non-finite values.
Results may differ from a plain program's by a relative error of at most 0.0029.
Values may be sent and summed in bfloat16 or wider, within the bound.
A program may use at most 64 MiB of HBM per device.

v0:
```python
import jax
import jax.numpy as jnp
from jax import lax
from jax.sharding import PartitionSpec as P

RHEADS = 32
NSEQ = 2
SEQ = 4096


def spread_heads(queries, heads, copies):
    rows = queries.shape[0]
    width = queries.shape[1] // heads
    shaped = queries.reshape(rows, heads, 1, width)
    return jnp.broadcast_to(shaped, (rows, heads, copies, width)).reshape(
        rows, heads * copies, width
    )


def local(teacher_query, student_hidden, query_weight):
    heads_here = RHEADS // lax.axis_size("tp")
    copies = lax.axis_size("dp") // heads_here
    rows = teacher_query.shape[0]
    teacher_width = teacher_query.shape[1] // heads_here
    hidden_full = lax.all_gather(student_hidden, "tp", axis=1, tiled=True)
    teacher_send = spread_heads(teacher_query, heads_here, copies)
    projected = jnp.dot(
        hidden_full,
        lax.all_gather(query_weight, "dp", axis=0, tiled=True),
        preferred_element_type=jnp.float32,
    )
    student_query = projected.astype(jnp.bfloat16)
    student_width = student_query.shape[1] // heads_here
    student_send = spread_heads(student_query, heads_here, copies)
    teacher_all, student_all = (
        lax.all_to_all(teacher_send, "dp", split_axis=1, concat_axis=0, tiled=True),
        lax.all_to_all(student_send, "dp", split_axis=1, concat_axis=0, tiled=True),
    )
    total_rows = teacher_all.shape[0]
    teacher_all = teacher_all.reshape(total_rows, teacher_width)
    student_all = student_all.reshape(total_rows, student_width)
    teacher_scale = teacher_width ** (-0.5)
    student_scale = student_width ** (-0.5)
    query_rows = SEQ // copies
    first_row = lax.axis_index("dp") % copies * query_rows
    block = min(512, query_rows)
    blocks_each = query_rows // block

    def relation_step(step, carry):
        kl_store, grad_store = carry
        sequence = step // blocks_each
        offset = step % blocks_each * block
        base = sequence * SEQ
        start = base + first_row + offset
        teacher_keys = lax.dynamic_slice_in_dim(teacher_all, base, SEQ, 0)
        student_keys = lax.dynamic_slice_in_dim(student_all, base, SEQ, 0)
        teacher_rows = lax.dynamic_slice_in_dim(teacher_all, start, block, 0)
        student_rows = lax.dynamic_slice_in_dim(student_all, start, block, 0)
        teacher_scores = (
            lax.dot_general(
                teacher_rows,
                teacher_keys,
                (((1,), (1,)), ((), ())),
                preferred_element_type=jnp.float32,
            )
            * teacher_scale
        )
        student_scores = (
            lax.dot_general(
                student_rows,
                student_keys,
                (((1,), (1,)), ((), ())),
                preferred_element_type=jnp.float32,
            )
            * student_scale
        )
        teacher_log = jax.nn.log_softmax(teacher_scores, axis=-1)
        student_log = jax.nn.log_softmax(student_scores, axis=-1)
        teacher_prob = jnp.exp(teacher_log)
        divergence = jnp.sum(teacher_prob * (teacher_log - student_log), axis=-1)
        score_grad = (jnp.exp(student_log) - teacher_prob).astype(jnp.bfloat16)
        key_part = (
            lax.dot_general(
                score_grad,
                student_rows,
                (((0,), (0,)), ((), ())),
                preferred_element_type=jnp.float32,
            )
            * student_scale
        )
        row_part = (
            jnp.dot(score_grad, student_keys, preferred_element_type=jnp.float32) * student_scale
        )
        seq_grad = lax.dynamic_slice_in_dim(grad_store, base, SEQ, 0)
        grad_store = lax.dynamic_update_slice_in_dim(grad_store, seq_grad + key_part, base, 0)
        current = lax.dynamic_slice_in_dim(grad_store, start, block, 0)
        grad_store = lax.dynamic_update_slice_in_dim(grad_store, current + row_part, start, 0)
        kl_store = lax.dynamic_update_slice_in_dim(
            kl_store, divergence, sequence * query_rows + offset, 0
        )
        return (kl_store, grad_store)

    kl_init = jnp.zeros((NSEQ * query_rows,), jnp.float32)
    grad_init = jnp.zeros((total_rows, student_width), jnp.float32)
    kl_store, grad_store = lax.fori_loop(0, NSEQ * blocks_each, relation_step, (kl_init, grad_init))
    returned = lax.all_to_all(
        grad_store.reshape(heads_here * copies, rows, student_width),
        "dp",
        split_axis=0,
        concat_axis=2,
        tiled=True,
    )
    summed = jnp.sum(returned.reshape(rows, heads_here, copies, student_width), axis=2)
    query_grad = summed.reshape(rows, heads_here * student_width).astype(jnp.bfloat16)
    weight_grad = lax.psum_scatter(
        lax.dot_general(
            hidden_full, query_grad, (((0,), (0,)), ((), ())), preferred_element_type=jnp.float32
        ),
        "dp",
        scatter_dimension=0,
        tiled=True,
    )
    return (kl_store.reshape(1, NSEQ * query_rows), weight_grad)


def solution(mesh):
    placed = (P("dp", "tp"), P("dp", "tp"), P("dp", "tp"))
    return jax.shard_map(
        local,
        mesh=mesh,
        in_specs=placed,
        out_specs=(P(("tp", "dp"), None), P("dp", "tp")),
        check_vma=False,
    )
```

profile of v0, /device:TPU:0, one launch (start us, length us, event | category | flops | bytes accessed | tf_op | source)
XLA Modules:
  0.0 1073.3 jit_solution(3401739146928426548)
XLA Ops:
  8.6 61.9 %all-gather.3.cloned.1.call-done = bf16[1024,4096]{1,0:T(8,128)(2,1)} async-done(((bf16[1024,1024]{1,0:T(8,128)(2,1)}), bf16[1024,4096]{1,0:T(8,128)(2,1)}) %all-gather.3.cloned.1.call-update) | async-done | bytes 8388624 | tf_op jit(solution)/shard_map/all_gather | solution.py:25
  70.6 126.6 %all-gather.5.cloned.1.call-done = bf16[4096,1024]{1,0:T(8,128)(2,1)} async-done(((bf16[512,1024]{1,0:T(8,128)(2,1)}), bf16[4096,1024]{1,0:T(8,128)(2,1)}) %all-gather.5.cloned.1.call-update) | async-done | bytes 8388624 | tf_op jit(solution)/shard_map/all_gather | solution.py:29
  197.2 14.7 %convolution_convert_fusion = bf16[1024,1024]{0,1:T(8,128)(2,1)} fusion(bf16[1024,4096]{1,0:T(8,128)(2,1)} %all-gather.3.cloned.1.call-done, bf16[4096,1024]{1,0:T(8,128)(2,1)} %all-gather.5.cloned.1.call-done), kind=kOutput, calls=%fused_computation.30 | convolution fusion | flops 8590983168 | bytes 18874368 | tf_op jit(solution)/shard_map/dot_general | solution.py:27
  219.9 43.3 %all-to-all-done.1 = bf16[1024,8,128]{0,2,1:T(8,128)(2,1)S(1)} async-done(((bf16[1024,8,128]{0,2,1:T(8,128)(2,1)}), bf16[1024,8,128]{0,2,1:T(8,128)(2,1)S(1)}, u32[]{:S(2)}, u32[]{:S(2)}) %all-to-all-start.1) | async-done | bytes 2097184 | tf_op jit(solution)/shard_map/all_to_all | solution.py:37
  271.1 89.3 %all-to-all-done = bf16[1024,8,256]{2,0,1:T(8,128)(2,1)} async-done(((bf16[1024,8,256]{2,0,1:T(8,128)(2,1)}), bf16[1024,8,256]{2,0,1:T(8,128)(2,1)}, u32[]{:S(2)}, u32[]{:S(2)}) %all-to-all-start) | async-done | bytes 4194336 | tf_op jit(solution)/shard_map/all_to_all | solution.py:36
  362.5 350.1 %while.17 = (s32[]{:T(128)}, f32[8192]{0:T(1024)S(1)}, f32[8192,128]{1,0:T(8,128)}, bf16[8192,256]{1,0:T(8,128)(2,1)}, bf16[8192,128]{1,0:T(8,128)(2,1)S(1)}, /*...) while((s32[]{:T(128)}, f32[8192]{0:T(1024)S(1)}, ...), condition=%wide.region_4.6_spmd, body=%wide.region_0.5_spmd.sunk | while | flops 2729571840 | bytes 89164200 | solution.py:105
  370.0 5.7 subtract_convert_fusion.2
  391.9 5.7 subtract_convert_fusion.2
  413.8 5.7 subtract_convert_fusion.2
  435.8 5.7 subtract_convert_fusion.2
  457.7 5.7 subtract_convert_fusion.2
  479.6 5.7 subtract_convert_fusion.2
  501.5 5.7 subtract_convert_fusion.2
  523.4 5.7 subtract_convert_fusion.2
  545.3 5.7 subtract_convert_fusion.2
  567.2 5.7 subtract_convert_fusion.2
  589.0 5.7 subtract_convert_fusion.2
  610.9 5.7 subtract_convert_fusion.2
  632.7 5.7 subtract_convert_fusion.2
  654.5 5.7 subtract_convert_fusion.2
  698.2 5.7 subtract_convert_fusion.2
  715.2 51.9 %all_to_all.39 = bf16[8,1024,128]{2,1,0:T(8,128)(2,1)} all-to-all(bf16[8,1024,128]{2,1,0:T(8,128)(2,1)S(1)} %convert.2), channel_id=1, replica_groups=mesh['tp'=4,'dp'=8] {'dp'}, dimensions={0} | all-to-all | bytes 4194304 | tf_op jit(solution)/shard_map/all_to_all | solution.py:106
  769.9 14.5 %convolution_bitcast_fusion = f32[4096,1024]{0,1:T(8,128)} fusion(bf16[1024,1024]{0,1:T(8,128)(2,1)S(1)} %bitcast.41, bf16[1024,4096]{1,0:T(8,128)(2,1)} %all-gather.3.cloned.1.call-done), kind=kOutput, calls=%fused_computation.27 | convolution fusion | flops 8589934592 | bytes 27262976 | tf_op jit(solution)/shard_map/dot_general | solution.py:116
  784.4 279.4 %reduce-scatter.2.cloned.1.call-done = f32[512,1024]{0,1:T(8,128)} async-done(((f32[4096,1024]{0,1:T(8,128)}), f32[512,1024]{0,1:T(8,128)}) %reduce-scatter.2.cloned.1.call-update) | async-done | bytes 2097168 | tf_op jit(solution)/shard_map/reduce_scatter | solution.py:115
  (196 shorter events, 292.1 us)
Async XLA Ops:
  7.2 63.4 %all-gather.3.cloned.1.call-start = ((), (), s32[]{:S(2)}) async-start(), calls=%async_computation.4 | async-start | bytes 10485760 | tf_op jit(solution)/shard_map/all_gather | solution.py:25
  7.9 189.3 %all-gather.5.cloned.1.call-start = ((), (), s32[]{:S(2)}) async-start(), calls=%async_computation.5 | async-start | bytes 9437184 | tf_op jit(solution)/shard_map/all_gather | solution.py:29
  211.9 51.3 %all-to-all-start.1 = ((bf16[1024,8,128]{0,2,1:T(8,128)(2,1)}), bf16[1024,8,128]{0,2,1:T(8,128)(2,1)S(1)}, u32[]{:S(2)}, u32[]{:S(2)}) async-start(bf16[1024,8,128]{0,2,1:T(8,128)(2,1)} %bitcast.40), calls=%async_computation.1 | async-start | bytes 4194304 | tf_op jit(solution)/shard_map/all_to_all | solution.py:37
  263.2 4.8 copy-start.1
  263.2 97.1 %all-to-all-start = ((bf16[1024,8,256]{2,0,1:T(8,128)(2,1)}), bf16[1024,8,256]{2,0,1:T(8,128)(2,1)}, u32[]{:S(2)}, u32[]{:S(2)}) async-start(bf16[1024,8,256]{2,0,1:T(8,128)(2,1)} %bitcast.36), calls=%async_computation | async-start | bytes 8388608 | tf_op jit(solution)/shard_map/all_to_all | solution.py:36
  267.8 796.1 %reduce-scatter.2.cloned.1.call-start = ((), (), s32[]{:S(2)}) async-start(), calls=%async_computation.6 | async-start | bytes 18874368 | tf_op jit(solution)/shard_map/reduce_scatter | solution.py:115
  375.9 5.7 copy-start
  397.8 5.7 copy-start
  419.7 5.7 copy-start
  441.7 5.7 copy-start
  463.6 5.7 copy-start
  485.5 5.7 copy-start
  507.4 5.7 copy-start
  529.3 5.7 copy-start
  551.2 5.6 copy-start
  573.1 5.6 copy-start
  594.9 5.6 copy-start
  616.8 5.6 copy-start
  638.6 5.6 copy-start
  660.4 5.6 copy-start
  682.3 5.6 copy-start
  704.1 5.6 copy-start
  712.6 71.8 %copy-start.2 = (f32[8192]{0:T(1024)}, f32[8192]{0:T(1024)S(1)}, u32[]{:S(2)}) copy-start(f32[8192]{0:T(1024)S(1)} %get-tuple-element.157) | copy-start | bytes 98308
Sparse Core Ops, SparseCore 0:
  9.5 60.9 all-gather.2
  72.7 124.4 all-gather.4
  784.6 279.2 reduce-scatter.1
where the time goes:
time: 1070 us
  waiting for transfers between devices  602 us (56%)
  matrix products  236 us (22%)
  other arithmetic  142 us (13%)
  blocking collectives  51.9 us (5%)
  local copies, waits for them, and re-layouts  18.6 us (2%)
  between operations  13.8 us (1%)
    reduce_scatter x1, waiting for transfers between devices, local(): lax.psum_scatter(lax.dot_general(hidden_full, query_grad, (((0,), (0,)),...  279 us
    all_gather x1, waiting for transfers between devices, local(): lax.all_gather(query_weight, 'dp', axis=0, tiled=True)  127 us
    convert_element_type x16, other arithmetic, relation_step(): score_grad = (jnp.exp(student_log) - teacher_prob).astype(jnp.bfloat16)  91.3 us
    dot_general x16, matrix products, relation_step(): lax.dot_general(score_grad, student_rows, (((0,), (0,)), ((), ())), prefe...  90 us
    all_to_all x1, waiting for transfers between devices, local(): lax.all_to_all(teacher_send, 'dp', split_axis=1, concat_axis=0, tiled=True)  89.3 us
    all_gather x1, waiting for transfers between devices, local(): hidden_full = lax.all_gather(student_hidden, 'tp', axis=1, tiled=True)  61.9 us
    all_to_all x1, blocking collectives, local(): lax.all_to_all(grad_store.reshape(heads_here * copies, rows, student_widt...  51.9 us
    dot_general x16, matrix products, relation_step(): lax.dot_general(teacher_rows, teacher_keys, (((1,), (1,)), ((), ())), pre...  49 us
  transfers between devices with their start and end apart: 5, of which 5 were waited for; matrix products, arithmetic and copies ran while one was open for 1% of the time, Pallas kernels for 0%

commit v1 on v0

--- a/solution.py
+++ b/solution.py
@@ -1,6 +1,11 @@
+import functools
+import math
+
 import jax
 import jax.numpy as jnp
 from jax import lax
+from jax.experimental import pallas as pl
+from jax.experimental.pallas import tpu as pltpu
 from jax.sharding import PartitionSpec as P
 
 RHEADS = 32
@@ -16,10 +21,157 @@
         rows, heads * copies, width
     )
 
+LOG2E = 1.0 / math.log(2.0)
+LN2 = math.log(2.0)
+LANES = 128
+
+
+def relation_body(
+    t_rows, t_keys, s_rows, s_keys, s_rows_t, kl_out, grad_out, t_buf, s_buf, g_buf, row_acc, key_acc,
+    *, group, chunk, t_scale, s_scale,
+):
+    step = pl.program_id(0)
+    block = t_rows.shape[0]
+    keys = t_keys.shape[0]
+    nt = (((1,), (1,)), ((), ()))
+
+    for c in range(keys // chunk):
+        at = slice(c * chunk, (c + 1) * chunk)
+        t_buf[:, at] = lax.dot_general(t_rows[...], t_keys[at, :], nt, preferred_element_type=jnp.float32)
+        s_buf[:, at] = lax.dot_general(s_rows[...], s_keys[at, :], nt, preferred_element_type=jnp.float32)
+
+    tiles = keys // LANES
+    ct = t_scale * LOG2E
+    cs = s_scale * LOG2E
+
+    def rows_of(i, carry):
+        at = pl.ds(pl.multiple_of(i * group, group), group)
+        t_max = t_buf[at, 0:LANES]
+        s_max = s_buf[at, 0:LANES]
+        for k in range(1, tiles):
+            cols = slice(k * LANES, (k + 1) * LANES)
+            t_max = jnp.maximum(t_max, t_buf[at, cols])
+            s_max = jnp.maximum(s_max, s_buf[at, cols])
+        t_max = jnp.broadcast_to(jnp.max(t_max, axis=1, keepdims=True), (group, LANES))
+        s_max = jnp.broadcast_to(jnp.max(s_max, axis=1, keepdims=True), (group, LANES))
+        t_sum = jnp.zeros((group, LANES), jnp.float32)
+        s_sum = jnp.zeros((group, LANES), jnp.float32)
+        gap = jnp.zeros((group, LANES), jnp.float32)
+        for k in range(tiles):
+            cols = slice(k * LANES, (k + 1) * LANES)
+            u = (t_buf[at, cols] - t_max) * ct
+            v = (s_buf[at, cols] - s_max) * cs
+            t_exp = jnp.exp2(u)
+            s_exp = jnp.exp2(v)
+            t_buf[at, cols] = t_exp
+            s_buf[at, cols] = s_exp
+            t_sum = t_sum + t_exp
+            s_sum = s_sum + s_exp
+            gap = gap + t_exp * (u - v)
+        t_sum = jnp.sum(t_sum, axis=1, keepdims=True)
+        s_sum = jnp.sum(s_sum, axis=1, keepdims=True)
+        gap = jnp.sum(gap, axis=1, keepdims=True)
+        kl = gap * LN2 / t_sum - jnp.log(t_sum) + jnp.log(s_sum)
+        kl_out[0, at, :] = jnp.broadcast_to(kl, (group, LANES))
+        t_inv = jnp.broadcast_to(1.0 / t_sum, (group, LANES))
+        s_inv = jnp.broadcast_to(1.0 / s_sum, (group, LANES))
+        for k in range(tiles):
+            cols = slice(k * LANES, (k + 1) * LANES)
+            g_buf[at, cols] = (s_buf[at, cols] * s_inv - t_buf[at, cols] * t_inv).astype(jnp.bfloat16)
+        return carry
+
+    lax.fori_loop(0, block // group, rows_of, 0)
+
+    @pl.when(step == 0)
+    def _():
+        key_acc[...] = jnp.zeros_like(key_acc)
+
+    row_acc[pl.ds(pl.multiple_of(step * block, block), block), :] = jnp.dot(
+        g_buf[...], s_keys[...], preferred_element_type=jnp.float32
+    )
+    for c in range(keys // chunk):
+        at = slice(c * chunk, (c + 1) * chunk)
+        key_acc[:, at] += jnp.dot(s_rows_t[...], g_buf[:, at], preferred_element_type=jnp.float32)
+
+    @pl.when(step == pl.num_programs(0) - 1)
+    def _():
+        def finish(c, carry):
+            at = pl.ds(pl.multiple_of(c * LANES, LANES), LANES)
+            grad_out[at, :] = ((row_acc[at, :] + key_acc[:, at].T) * s_scale).astype(jnp.bfloat16)
+            return carry
+
+        lax.fori_loop(0, keys // LANES, finish, 0)
+
+
+def relation(teacher, student):
+    keys, t_width = teacher.shape
+    s_width = student.shape[1]
+    block = min(256, keys)
+    group = 16
+    chunk = min(1024, keys)
+    steps = keys // block
+    kl, grad = pl.pallas_call(
+        functools.partial(
+            relation_body, group=group, chunk=chunk, t_scale=t_width ** (-0.5), s_scale=s_width ** (-0.5)
+        ),
+        grid=(steps,),
+        in_specs=[
+            pl.BlockSpec((block, t_width), lambda i: (i, 0)),
+            pl.BlockSpec((keys, t_width), lambda i: (0, 0)),
+            pl.BlockSpec((block, s_width), lambda i: (i, 0)),
+            pl.BlockSpec((keys, s_width), lambda i: (0, 0)),
+            pl.BlockSpec((s_width, block), lambda i: (0, i)),
+        ],
+        out_specs=[
+            pl.BlockSpec((1, block, LANES), lambda i: (i, 0, 0)),
+            pl.BlockSpec((keys, s_width), lambda i: (0, 0)),
+        ],
+        out_shape=[
+            jax.ShapeDtypeStruct((steps, block, LANES), jnp.float32),
+            jax.ShapeDtypeStruct((keys, s_width), jnp.bfloat16),
+        ],
+        scratch_shapes=[
+            pltpu.VMEM((block, keys), jnp.float32),
+            pltpu.VMEM((block, keys), jnp.float32),
+            pltpu.VMEM((block, keys), jnp.bfloat16),
+            pltpu.VMEM((keys, s_width), jnp.float32),
+            pltpu.VMEM((s_width, keys), jnp.float32),
+        ],
+        compiler_params=pltpu.CompilerParams(
+            dimension_semantics=("arbitrary",), vmem_limit_bytes=40 * 1024 * 1024
+        ),
+        name="relation",
+    )(teacher, teacher, student, student, student.T)
+    return kl[:, :, 0].reshape(keys), grad
+
+
+def whole_heads(teacher_query, student_hidden, query_weight):
+    width = teacher_query.shape[1] // lax.axis_size("dp")
+    teacher_all = lax.all_to_all(teacher_query, "dp", split_axis=1, concat_axis=0, tiled=True)
+    hidden_full = lax.all_gather(student_hidden, "tp", axis=1, tiled=True)
+    weight_full = lax.all_gather(query_weight, "dp", axis=0, tiled=True)
+    student_query = jnp.dot(hidden_full, weight_full, preferred_element_type=jnp.float32).astype(jnp.bfloat16)
+    student_all = lax.all_to_all(student_query, "dp", split_axis=1, concat_axis=0, tiled=True)
+    hidden_cols = lax.all_to_all(hidden_full, "dp", split_axis=1, concat_axis=0, tiled=True)
+    kls = []
+    total = None
+    for s in range(NSEQ):
+        at = slice(s * SEQ, (s + 1) * SEQ)
+        kl, grad = relation(teacher_all[at], student_all[at])
+        kls.append(kl)
+        grads = lax.all_gather(grad, "dp", axis=1, tiled=True)
+        part = lax.dot_general(
+            hidden_cols[at], grads, (((0,), (0,)), ((), ())), preferred_element_type=jnp.float32
+        )
+        total = part if total is None else total + part
+    return jnp.concatenate(kls).reshape(1, NSEQ * SEQ), total
+
 
 def local(teacher_query, student_hidden, query_weight):
     heads_here = RHEADS // lax.axis_size("tp")
     copies = lax.axis_size("dp") // heads_here
+    if copies == 1 and heads_here == lax.axis_size("dp"):
+        return whole_heads(teacher_query, student_hidden, query_weight)
     rows = teacher_query.shape[0]
     teacher_width = teacher_query.shape[1] // heads_here
     hidden_full = lax.all_gather(student_hidden, "tp", axis=1, tiled=True)

time: 1070 us -> 847 us (0.79)
  Pallas kernels: 0 us -> 246 us
  matrix products: 236 us -> 34.9 us
  other arithmetic: 142 us -> 0.62 us
  waiting for transfers between devices: 602 us -> 481 us
  blocking collectives: 51.9 us -> 0 us
  local copies, waits for them, and re-layouts: 18.6 us -> 52.6 us
    reduce_scatter x1 -> x0, waiting for transfers between devices: 279 us -> none  [local(): lax.psum_scatter(lax.dot_general(hidden_full, query_grad, (((0,), (0,)),...]
    pallas_call x0 -> x2, Pallas kernels: none -> 246 us  [relation(): pl.pallas_call(functools.partial(relation_body, group=group, chunk=chunk,...]
    dot_general x66 -> x3, matrix products: 236 us -> 34.9 us  [the longest x2 20.2 us: whole_heads(): lax.dot_general(hidden_cols[at], grads, (((0,), (0,)), ((), ())), preferr...]
    all_gather x2 -> x4, waiting for transfers between devices: 189 us -> 286 us  [the longest x1 151 us: whole_heads(): weight_full = lax.all_gather(query_weight, 'dp', axis=0, tiled=True)]
    convert_element_type x16 -> x0, other arithmetic: 91.3 us -> none  [relation_step(): score_grad = (jnp.exp(student_log) - teacher_prob).astype(jnp.bfloat16)]
    all_to_all x2 -> x3, waiting for transfers between devices: 133 us -> 194 us  [the longest x1 150 us: whole_heads(): lax.all_to_all(hidden_full, 'dp', split_axis=1, concat_axis=0, tiled=True)]
    all_to_all x1 -> x0, blocking collectives: 51.9 us -> none  [local(): lax.all_to_all(grad_store.reshape(heads_here * copies, rows, student_widt...]
    reduce_sum x32 -> x0, other arithmetic: 48.2 us -> none  [the longest x16 24.2 us: relation_step(): student_log = jax.nn.log_softmax(student_scores, axis=-1)]
  transfers between devices with their start and end apart: 5 -> 7, of which waited for: 5 -> 5; matrix products, arithmetic and copies ran while one was open for 1% -> 7% of each run, Pallas kernels for 0% -> 15%
where the time goes in v1:
time: 847 us; the launch traced here: 846 us
  waiting for transfers between devices  481 us (57%)
  Pallas kernels  246 us (29%)
  local copies, waits for them, and re-layouts  52.6 us (6%)
  matrix products  34.9 us (4%)
  starting transfers between devices  17.2 us (2%)
  between operations  13.9 us (2%)
    pallas_call x2, Pallas kernels, relation(): pl.pallas_call(functools.partial(relation_body, group=group, chunk=chunk,...  246 us
    all_gather x1, waiting for transfers between devices, whole_heads(): weight_full = lax.all_gather(query_weight, 'dp', axis=0, tiled=True)  151 us
    all_to_all x1, waiting for transfers between devices, whole_heads(): lax.all_to_all(hidden_full, 'dp', split_axis=1, concat_axis=0, tiled=True)  150 us
    all_gather x2, waiting for transfers between devices, whole_heads(): grads = lax.all_gather(grad, 'dp', axis=1, tiled=True)  86.2 us
    all_gather x1, waiting for transfers between devices, whole_heads(): hidden_full = lax.all_gather(student_hidden, 'tp', axis=1, tiled=True)  48.6 us
    all_to_all x1, waiting for transfers between devices, whole_heads(): lax.all_to_all(student_query, 'dp', split_axis=1, concat_axis=0, tiled=True)  43.9 us
    dot_general x2, matrix products, whole_heads(): lax.dot_general(hidden_cols[at], grads, (((0,), (0,)), ((), ())), preferr...  20.2 us
    slice x3, local copies, waits for them, and re-layouts, whole_heads(): hidden_cols[at]  18.7 us
  transfers between devices with their start and end apart: 7, of which 5 were waited for; matrix products, arithmetic and copies ran while one was open for 7% of the time, Pallas kernels for 15%

profile of v1, /device:TPU:0, one launch (start us, length us, event | category | flops | bytes accessed | tf_op | source)
XLA Modules:
  0.0 845.9 jit_solution(13697044965763636197)
XLA Ops:
  7.2 3.9 copy.30
  11.9 4.5 copy.46
  16.4 7.3 all-to-all-start
  23.7 48.6 %all-gather.5.cloned.1.call-done = bf16[1024,4096]{0,1:T(8,128)(2,1)} async-done(((bf16[1024,1024]{0,1:T(8,128)(2,1)}), bf16[1024,4096]{0,1:T(8,128)(2,1)}) %all-gather.5.cloned.1.call-update) | async-done | bytes 8388624 | tf_op jit(solution)/shard_map/all_gather | solution.py:151
  72.3 151.5 %all-gather.7.cloned.1.call-done = bf16[4096,1024]{1,0:T(8,128)(2,1)} async-done(((bf16[512,1024]{1,0:T(8,128)(2,1)}), bf16[4096,1024]{1,0:T(8,128)(2,1)}) %all-gather.7.cloned.1.call-update) | async-done | bytes 8388624 | tf_op jit(solution)/shard_map/all_gather | solution.py:152
  223.8 14.7 %convolution_convert_fusion = bf16[1024,1024]{0,1:T(8,128)(2,1)} fusion(bf16[1024,4096]{0,1:T(8,128)(2,1)} %all-gather.5.cloned.1.call-done, bf16[4096,1024]{1,0:T(8,128)(2,1)} %all-gather.7.cloned.1.call-done), kind=kOutput, calls=%fused_computation.4 | convolution fusion | flops 8590983168 | bytes 18874368 | tf_op jit(solution)/shard_map/dot_general | solution.py:153
  238.5 4.4 all-to-all-start.1
  242.9 3.8 fusion.1
  246.8 43.9 %all-to-all-done.1 = bf16[1024,8,128]{0,2,1:T(8,128)(2,1)} async-done(((bf16[1024,8,128]{0,2,1:T(8,128)(2,1)}), bf16[1024,8,128]{0,2,1:T(8,128)(2,1)}, u32[]{:S(2)}, u32[]{:S(2)}) %all-to-all-start.1) | async-done | bytes 2097184 | tf_op jit(solution)/shard_map/all_to_all | solution.py:154
  290.7 2.7 slice_bitcast_fusion.1
  294.5 1.6 copy.32.s_rows.s_keys
  298.9 122.9 %relation.2 = (f32[16,256,128]{2,1,0:T(8,128)S(1)}, bf16[4096,128]{1,0:T(8,128)(2,1)S(1)}) custom-call(bf16[4096,256]{1,0:T(8,128)(2,1)S(1)} %bitcast.38, bf16[4096,256]{1,0:T(8,128)(2,1)S(1)} %bitcast.39, bf16[4096,128]{1,0:T(8,128)(2,1)S(1)} %copy.32.s_rows.s_keys, bf16[4096,128]{1,0:T(8,128)(2,1)S(1)} %copy.32.s_rows.s_keys, bf16[128,4096]{1,0:T(8,128)(2,1)S(1)} %bitcast.43), custom_call_target="tpu_custom_call" | custom-call | tf_op jit(solution)/shard_map/relation/pallas_call | solution.py:113
  424.2 5.2 all-to-all-start.2
  430.7 1.7 copy.35.s_rows.s_keys
  433.7 122.9 %relation.3 = (f32[16,256,128]{2,1,0:T(8,128)S(1)}, bf16[4096,128]{1,0:T(8,128)(2,1)S(1)}) custom-call(bf16[4096,256]{1,0:T(8,128)(2,1)S(1)} %bitcast.36, bf16[4096,256]{1,0:T(8,128)(2,1)S(1)} %bitcast.37, bf16[4096,128]{1,0:T(8,128)(2,1)S(1)} %copy.35.s_rows.s_keys, bf16[4096,128]{1,0:T(8,128)(2,1)S(1)} %copy.35.s_rows.s_keys, bf16[128,4096]{1,0:T(8,128)(2,1)S(1)} %bitcast.41), custom_call_target="tpu_custom_call" | custom-call | tf_op jit(solution)/shard_map/relation/pallas_call | solution.py:113
  558.9 2.3 slice_reduce_fusion
  562.5 150.0 %all-to-all-done.2 = bf16[1024,8,512]{0,2,1:T(8,128)(2,1)} async-done(((bf16[1024,8,512]{0,2,1:T(8,128)(2,1)}), bf16[1024,8,512]{0,2,1:T(8,128)(2,1)}, u32[]{:S(2)}, u32[]{:S(2)}) %all-to-all-start.2) | async-done | bytes 8388640 | tf_op jit(solution)/shard_map/all_to_all | solution.py:155
  712.5 6.2 fusion
  718.7 6.3 copy.37
  725.0 6.2 copy.38
  731.2 10.4 %fusion.2 = f32[1024,512]{1,0:T(8,128)} fusion(bf16[4096,1024]{1,0:T(8,128)(2,1)} %all-gather.9.cloned.1.call-done, bf16[4096,512]{1,0:T(8,128)(2,1)} %bitcast.48), kind=kOutput, calls=%fused_computation.10 | convolution fusion | flops 4294967296 | bytes 14680064 | tf_op jit(solution)/shard_map/dot_general | solution.py:163
  741.6 86.2 %all-gather.11.cloned.1.call-done = bf16[4096,1024]{1,0:T(8,128)(2,1)} async-done(((bf16[4096,128]{1,0:T(8,128)(2,1)}), bf16[4096,1024]{1,0:T(8,128)(2,1)}) %all-gather.11.cloned.1.call-update) | async-done | bytes 8388624 | tf_op jit(solution)/shard_map/all_gather | solution.py:162
  827.8 9.8 %add_bitcast_fusion = f32[512,1024]{0,1:T(8,128)S(1)} fusion(f32[1024,512]{1,0:T(8,128)} %fusion.2, bf16[4096,1024]{1,0:T(8,128)(2,1)} %all-gather.11.cloned.1.call-done, bf16[4096,512]{1,0:T(8,128)(2,1)} %bitcast.47), kind=kOutput, calls=%fused_computation.1 | convolution fusion | flops 4295491584 | bytes 16777216 | tf_op jit(solution)/shard_map/dot_general | solution.py:163
  837.6 1.8 copy.39
  (34 shorter events, 13.2 us)
Async XLA Ops:
  7.2 65.2 %all-gather.5.cloned.1.call-start = ((), (), s32[]{:S(2)}) async-start(), calls=%async_computation.3 | async-start | bytes 10485760 | tf_op jit(solution)/shard_map/all_gather | solution.py:151
  11.2 212.6 %all-gather.7.cloned.1.call-start = ((), (), s32[]{:S(2)}) async-start(), calls=%async_computation.4 | async-start | bytes 9437184 | tf_op jit(solution)/shard_map/all_gather | solution.py:152
  16.4 222.1 %all-to-all-start = ((bf16[1024,8,256]{2,0,1:T(8,128)(2,1)}), bf16[1024,8,256]{2,0,1:T(8,128)(2,1)}, u32[]{:S(2)}, u32[]{:S(2)}) async-start(bf16[1024,8,256]{2,0,1:T(8,128)(2,1)} %bitcast.44), calls=%async_computation | async-start | bytes 8388608 | tf_op jit(solution)/shard_map/all_to_all | solution.py:150
  238.5 52.2 %all-to-all-start.1 = ((bf16[1024,8,128]{0,2,1:T(8,128)(2,1)}), bf16[1024,8,128]{0,2,1:T(8,128)(2,1)}, u32[]{:S(2)}, u32[]{:S(2)}) async-start(bf16[1024,8,128]{0,2,1:T(8,128)(2,1)} %bitcast.2), calls=%async_computation.1 | async-start | bytes 4194304 | tf_op jit(solution)/shard_map/all_to_all | solution.py:154
  242.9 488.3 %all-gather.9.cloned.1.call-start = ((), (), s32[]{:S(2)}) async-start(), calls=%async_computation.5 | async-start | bytes 9437184 | tf_op jit(solution)/shard_map/all_gather | solution.py:162
  296.1 1.6 copy-start
  297.7 1.2 copy-start.2
  421.9 1.3 copy-start.3
  423.2 1.0 copy-start.6
  424.2 5.4 copy-start.8
  424.2 288.3 %all-to-all-start.2 = ((bf16[1024,8,512]{0,2,1:T(8,128)(2,1)}), bf16[1024,8,512]{0,2,1:T(8,128)(2,1)}, u32[]{:S(2)}, u32[]{:S(2)}) async-start(bf16[1024,8,512]{0,2,1:T(8,128)(2,1)} %bitcast.45), calls=%async_computation.2 | async-start | bytes 16777216 | tf_op jit(solution)/shard_map/all_to_all | solution.py:155
  429.4 398.4 %all-gather.11.cloned.1.call-start = ((), (), s32[]{:S(2)}) async-start(), calls=%async_computation.6 | async-start | bytes 9437184 | tf_op jit(solution)/shard_map/all_gather | solution.py:162
  432.4 1.3 copy-start.1
  556.6 1.3 copy-start.5
  557.9 1.0 copy-start.7
  558.9 2.4 copy-start.4
Sparse Core Ops, SparseCore 0:
  11.3 60.9 all-gather.4
  74.4 149.3 all-gather.6
  424.3 278.3 all-gather.8
  704.6 123.1 all-gather.10
